TPU v7x, 32 devices: a whole 2x2x4 slice. The times are simulated.
32 devices in a mesh: row: 8 (over z, x), col: 4 (over y, core).
Axes of the slice: x: 2, y: 2, z: 4, core: 2. Of those that a mesh axis runs over, the one named last changes fastest.
Arguments:
- field: bfloat16 [192, 128, 256], P('row', 'col'), may hold values from -6 to 6
- gains: float32 [1, 2, 256], replicated, may hold values from 0.5 to 1.5
- w_query: bfloat16 [1, 256, 256], replicated, may hold values from -24 to 24
- w_key: bfloat16 [1, 256, 256], replicated, may hold values from -1 to 1
- w_value: bfloat16 [1, 256, 256], replicated, may hold values from -0.375 to 0.375
- w_out: bfloat16 [1, 256, 256], replicated, may hold values from -0.375 to 0.375
- w_up: bfloat16 [1, 256, 1024], replicated, may hold values from -0.375 to 0.375
- w_down: bfloat16 [1, 1024, 256], replicated, may hold values from -0.1875 to 0.1875
- final_gain: float32 [256], replicated, may hold values from 0.5 to 1.5
- conv_weight: bfloat16 [3, 3, 256, 256], replicated, may hold values from -0.125 to 0.125
Outputs:
- image: float32 [16, 768, 512], P(None, 'row', 'col')
All inputs are finite; a program needn't handle non-finite values.
Results may differ from a plain program's by a relative error of at most 0.0056.
Values may be sent and summed in bfloat16 or wider, within the bound.
A program may use at most 64 MiB of HBM per device.

v0:
```python
import functools

import jax
import jax.numpy as jnp
from jax import lax
from jax.experimental import pallas as pl
from jax.experimental.pallas import tpu as pltpu
from jax.sharding import PartitionSpec as P

HEADS = 8
HALO = 8
SHUF = 4
CHUNK = 256
VMEM_LIMIT = 56 * 1024 * 1024
BF = jnp.bfloat16
F32 = jnp.float32
NEIGHBOURS = ((-1, 0), (1, 0), (0, -1), (0, 1), (-1, -1), (-1, 1), (1, -1), (1, 1))


def rms(values, gain):
    return values * lax.rsqrt(jnp.mean(values * values, axis=-1, keepdims=True) + 1e-06) * gain


def there(step, sizes):
    row, col = lax.axis_index("row"), lax.axis_index("col")
    nrow, ncol = row + step[0], col + step[1]
    ok = (nrow >= 0) & (nrow < sizes[0]) & (ncol >= 0) & (ncol < sizes[1])
    return ok, nrow, ncol


def greet(sizes):
    barrier = pltpu.get_barrier_semaphore()
    for step in NEIGHBOURS:
        ok, nrow, ncol = there(step, sizes)

        @pl.when(ok)
        def _():
            pl.semaphore_signal(
                barrier, inc=1, device_id=(nrow, ncol), device_id_type=pl.DeviceIdType.MESH
            )

    peers = jnp.int32(0)
    for step in NEIGHBOURS:
        peers = peers + there(step, sizes)[0].astype(jnp.int32)
    pl.semaphore_wait(barrier, peers)


def swap(sizes, sources, slots, send, recv, fills):
    copies = []
    for n, step in enumerate(NEIGHBOURS):
        ok, nrow, ncol = there(step, sizes)
        back = NEIGHBOURS.index((-step[0], -step[1]))
        copy = pltpu.make_async_remote_copy(
            src_ref=sources[n],
            dst_ref=slots[back],
            send_sem=send.at[n],
            recv_sem=recv.at[back],
            device_id=(nrow, ncol),
            device_id_type=pl.DeviceIdType.MESH,
        )
        arrival = pltpu.make_async_remote_copy(
            src_ref=slots[n],
            dst_ref=slots[n],
            send_sem=send.at[n],
            recv_sem=recv.at[n],
            device_id=(nrow, ncol),
            device_id_type=pl.DeviceIdType.MESH,
        )
        copies.append((ok, copy, arrival))
        pl.when(ok)(copy.start)
        pl.when(jnp.logical_not(ok))(fills[n])
    return copies


def finish(copies):
    for ok, copy, arrival in copies:
        pl.when(ok)(arrival.wait_recv)
    for ok, copy, _ in copies:
        pl.when(ok)(copy.wait_send)


def pieces(rows, groups):
    return [HALO * groups] * 2 + [rows] * 2 + [HALO] * 4


def halo_start(sizes, field_ref, halo_ref, send, recv):
    rows, groups = field_ref.shape[:2]
    sources, slots, fills = [], [], []
    first = 0
    for step, count in zip(NEIGHBOURS, pieces(rows, groups)):
        dr, dc = step
        rsel = slice(0, rows) if dr == 0 else (slice(0, HALO) if dr < 0 else slice(rows - HALO, rows))
        slot = halo_ref.at[pl.ds(first, count)]
        if dc == 0:
            sources.append(field_ref.at[rsel])
            slots.append(slot.reshape(HALO, groups, 8, field_ref.shape[3]))
        else:
            sources.append(field_ref.at[rsel, 0 if dc < 0 else groups - 1])
            slots.append(slot)

        def fill(first=first, count=count):
            for k in range(0, count, HALO):
                halo_ref[first + k : first + k + HALO] = field_ref[0:HALO, 0]

        fills.append(fill)
        first += count
    return swap(sizes, sources, slots, send, recv, fills)


def layer_kernel(
    sizes,
    field_ref, gains_ref, wq_ref, wk_ref, wv_ref, wo_hbm, wu_hbm, wd_hbm, fg_ref,
    out_ref, row_h, col_h, cor_h,
    halo_ref, q_s, kt_s, va_s, f_s, o_s, m_s, left_s, right_s, wo_ref, wu_ref, wd_ref,
    send, recv, send2, recv2, wsem,
):
    rows, groups = field_ref.shape[:2]
    cols = groups * 8
    tokens, width = q_s.shape
    head = width // HEADS
    per = 128 // head
    loads = [
        pltpu.make_async_copy(src, dst, wsem.at[n])
        for n, (src, dst) in enumerate(((wo_hbm, wo_ref), (wu_hbm, wu_ref), (wd_hbm, wd_ref)))
    ]
    for load in loads:
        load.start()
    greet(sizes)
    copies = halo_start(sizes, field_ref, halo_ref, send, recv)

    g0 = gains_ref[0:1, :]
    g1 = gains_ref[1:2, :]
    fg = fg_ref[...]
    lane = lax.broadcasted_iota(jnp.int32, (1, 128), 1) // head

    def keep(h, start, ok):
        k = jnp.dot(h, wk_ref[...], preferred_element_type=F32)
        kt_s[:, start : start + h.shape[0]] = k.T.astype(BF)
        v = jnp.dot(h, wv_ref[...], preferred_element_type=F32)
        for e in range(HEADS):
            half = e // per
            part = jnp.where(lane == e % per, v[:, half * 128 : half * 128 + 128], 1.0)
            if ok is not None:
                part = part * ok
            va_s[e, start : start + h.shape[0], :] = part.astype(BF)

    scale = head**-0.5 * 1.4426950408889634
    span = CHUNK // cols
    for start in range(0, tokens, CHUNK):
        at = start // cols
        h = rms(field_ref[at : at + span].astype(F32).reshape(CHUNK, width), g0).astype(BF)
        q = jnp.dot(h, wq_ref[...], preferred_element_type=F32) * scale
        q_s[start : start + CHUNK, :] = q.astype(BF)
        keep(h, start, None)

    def head_part(at, half, e, first, count):
        qh = q_s[at, half * 128 : half * 128 + 128]
        qm = jnp.where(lane == e, qh, jnp.zeros_like(qh))
        keys = slice(first, first + count)
        s = jnp.dot(qm, kt_s[half * 128 : half * 128 + 128, keys], preferred_element_type=F32)
        m = jnp.max(s, axis=-1, keepdims=True)
        p = jnp.exp2((s - m).astype(BF))
        return m, jnp.dot(p, va_s[half * per + e, keys, :], preferred_element_type=F32)

    def own(index, carry):
        at = pl.ds(pl.multiple_of(index * CHUNK, CHUNK), CHUNK)
        for half in range(width // 128):
            for e in range(per):
                m, o = head_part(at, half, e, 0, tokens)
                o_s[half * per + e, at, :] = o
                m_s[half * per + e, at, :] = jnp.broadcast_to(m, o.shape)
        return carry

    lax.fori_loop(0, tokens // CHUNK, own, 0)
    finish(copies)

    first = 0
    marks = []
    for step, count in zip(NEIGHBOURS, pieces(rows, groups)):
        ok = there(step, sizes)[0].astype(F32)
        marks.append((first * 8, count * 8, ok))
        first += count
    total = first * 8
    for start in range(0, total, 128):
        raw = halo_ref[start // 8 : start // 8 + 16].astype(F32).reshape(128, width)
        h = rms(raw, g0).astype(BF)
        row = lax.broadcasted_iota(jnp.int32, (128, 1), 0) + start
        ok = jnp.zeros((128, 1), F32)
        for at, count, flag in marks:
            if at < start + 128 and at + count > start:
                ok = jnp.where((row >= at) & (row < at + count), flag, ok)
        keep(h, tokens + start, ok)
    for load in loads:
        load.wait()

    def body(index, carry):
        at = pl.ds(pl.multiple_of(index * CHUNK, CHUNK), CHUNK)
        halves = []
        for half in range(width // 128):
            ctx = jnp.zeros((CHUNK, 128), F32)
            for e in range(per):
                m, o = head_part(at, half, e, tokens, total)
                old = m_s[half * per + e, at, :]
                top = jnp.maximum(old, m)
                o = o * jnp.exp2(m - top) + o_s[half * per + e, at, :] * jnp.exp2(old - top)
                ctx = jnp.where(lane == e, o / pltpu.roll(o, head, 1), ctx)
            halves.append(ctx.astype(BF))
        ctx = jnp.concatenate(halves, axis=1)
        x = field_ref[pl.ds(index * span, span)].astype(F32).reshape(CHUNK, width)
        x = x + jnp.dot(ctx, wo_ref[...], preferred_element_type=F32)
        h = rms(x, g1).astype(BF)
        u = jax.nn.gelu(jnp.dot(h, wu_ref[...], preferred_element_type=F32)).astype(BF)
        x = x + jnp.dot(u, wd_ref[...], preferred_element_type=F32)
        f = rms(x, fg)
        out_ref[pl.ds(index * span, span)] = f.reshape(span, cols, width).astype(BF)
        for half in range(width // 128):
            f_s[half, at, :] = f[:, half * 128 : half * 128 + 128]
        return carry

    lax.fori_loop(0, tokens // CHUNK, body, 0)
    for half in range(width // 128):
        sl = slice(half * 128, half * 128 + 128)
        left_s[:, sl] = f_s[half, pl.ds(0, rows, stride=cols), :].astype(BF)
        right_s[:, sl] = f_s[half, pl.ds(cols - 1, rows, stride=cols), :].astype(BF)
    slots = [row_h.at[0], row_h.at[1], col_h.at[0], col_h.at[1]] + [cor_h.at[n] for n in range(4)]
    sources = [
        out_ref.at[0], out_ref.at[rows - 1], left_s, right_s,
        left_s.at[pl.ds(0, 8)], right_s.at[pl.ds(0, 8)],
        left_s.at[pl.ds(rows - 8, 8)], right_s.at[pl.ds(rows - 8, 8)],
    ]

    def filler(slot):
        def fill():
            slot[...] = jnp.zeros(slot.shape, BF)
        return fill

    finish(swap(sizes, sources, slots, send2, recv2, [filler(s) for s in slots]))


def layer(sizes, field, gains, wq, wk, wv, wo, wu, wd, fg):
    rows, cols, width = field.shape
    groups = cols // 8
    tokens = rows * cols
    blocks = sum(pieces(rows, groups))
    keys = tokens + blocks * 8
    vm = pl.BlockSpec(memory_space=pltpu.VMEM)
    hbm = pl.BlockSpec(memory_space=pl.ANY)
    eight = pltpu.SemaphoreType.DMA((8,))
    return pl.pallas_call(
        functools.partial(layer_kernel, sizes),
        out_shape=(
            jax.ShapeDtypeStruct((rows, cols, width), BF),
            jax.ShapeDtypeStruct((2, cols, width), BF),
            jax.ShapeDtypeStruct((2, rows, width), BF),
            jax.ShapeDtypeStruct((4, 8, width), BF),
        ),
        in_specs=[vm] * 5 + [hbm] * 3 + [vm],
        out_specs=(vm,) * 4,
        scratch_shapes=[
            pltpu.VMEM((blocks, 8, width), BF),
            pltpu.VMEM((tokens, width), BF),
            pltpu.VMEM((width, keys), BF),
            pltpu.VMEM((HEADS, keys, 128), BF),
            pltpu.VMEM((width // 128, tokens, 128), F32),
            pltpu.VMEM((HEADS, tokens, 128), F32),
            pltpu.VMEM((HEADS, tokens, 128), F32),
            pltpu.VMEM((rows, width), BF),
            pltpu.VMEM((rows, width), BF),
            pltpu.VMEM(wo.shape, BF),
            pltpu.VMEM(wu.shape, BF),
            pltpu.VMEM(wd.shape, BF),
            eight, eight, eight, eight,
            pltpu.SemaphoreType.DMA((3,)),
        ],
        compiler_params=pltpu.CompilerParams(
            collective_id=0, has_side_effects=True, vmem_limit_bytes=VMEM_LIMIT
        ),
        name="layer",
    )(field.reshape(rows, groups, 8, width), gains, wq, wk, wv, wo, wu, wd, fg)


def conv_kernel(final_ref, row_h, col_h, cor_h, weight_ref, image_ref, fb_s, wp_s, up_s):
    rows, cols, width = final_ref.shape
    tokens = rows * cols
    outs = weight_ref.shape[1]
    old = lax.broadcasted_iota(jnp.int32, (outs, outs), 0)
    new = lax.broadcasted_iota(jnp.int32, (outs, outs), 1)
    want = (new % (outs // SHUF)) * SHUF + new // (outs // SHUF)
    perm = jnp.where(old == want, 1.0, 0.0).astype(BF)
    for tap in range(9):
        sl = slice(tap * width, (tap + 1) * width)
        wp_s[sl, :] = jnp.dot(weight_ref[sl, :], perm, preferred_element_type=F32).astype(BF)
    col = lax.broadcasted_iota(jnp.int32, (1, cols, 1), 1)

    def spread(first, count, x, before, after):
        flat = x.reshape(count * cols, width)
        low = pltpu.roll(flat, 1, 0).reshape(count, cols, width)
        high = pltpu.roll(flat, count * cols - 1, 0).reshape(count, cols, width)
        fb_s[1, first : first + count] = x.astype(BF)
        fb_s[0, first : first + count] = jnp.where(col == 0, before, low).astype(BF)
        fb_s[2, first : first + count] = jnp.where(col == cols - 1, after, high).astype(BF)

    for r in range(0, rows, 8):
        before = col_h[0, r : r + 8, :].astype(F32)[:, None, :]
        after = col_h[1, r : r + 8, :].astype(F32)[:, None, :]
        spread(1 + r, 8, final_ref[r : r + 8].astype(F32), before, after)
    for side, at, pick in ((0, 0, 7), (1, rows + 1, 0)):
        before = cor_h[2 * side].astype(F32)[pick : pick + 1][:, None, :]
        after = cor_h[2 * side + 1].astype(F32)[pick : pick + 1][:, None, :]
        spread(at, 1, row_h[side].astype(F32)[None], before, after)

    step = 8
    quarter = outs // SHUF
    for r in range(0, rows, step):
        acc = jnp.zeros((step * cols, outs), F32)
        for a in range(3):
            for b in range(3):
                tap = a * 3 + b
                acc = acc + jnp.dot(
                    fb_s[b, r + a : r + a + step].reshape(step * cols, width),
                    wp_s[tap * width : (tap + 1) * width, :],
                    preferred_element_type=F32,
                )
        for k in range(step):
            part = acc[k * cols : (k + 1) * cols]
            slot = k % 2
            for j in range(SHUF):
                pair = j * quarter // 128
                up_s[slot, pl.ds(j, cols, stride=SHUF), :] = part[:, pair * 128 : pair * 128 + 128]
            t = up_s[slot].T
            lanes = lax.broadcasted_iota(jnp.int32, (1, cols * SHUF), 1)
            t = jnp.where(lanes % 2 == 0, t[:quarter], t[quarter : 2 * quarter])
            for c in range(quarter // SHUF):
                image_ref[c, (r + k) * SHUF : (r + k + 1) * SHUF, :] = t[c * SHUF : (c + 1) * SHUF]


def conv_image(final, row, col, corner, weight):
    rows, cols, width = final.shape
    outs = weight.shape[1]
    vm = pl.BlockSpec(memory_space=pltpu.VMEM)
    return pl.pallas_call(
        conv_kernel,
        out_shape=jax.ShapeDtypeStruct((outs // SHUF**2, rows * SHUF, cols * SHUF), F32),
        in_specs=[vm] * 5,
        out_specs=vm,
        scratch_shapes=[
            pltpu.VMEM((3, rows + 2, cols, width), BF),
            pltpu.VMEM(weight.shape, BF),
            pltpu.VMEM((2, cols * SHUF, 128), F32),
        ],
        compiler_params=pltpu.CompilerParams(vmem_limit_bytes=VMEM_LIMIT),
        name="conv_image",
    )(final, row, col, corner, weight)


def local(sizes, field, gains, w_query, w_key, w_value, w_out, w_up, w_down, final_gain, conv_weight):
    final, row, col, corner = layer(
        sizes, field, gains[0], w_query[0], w_key[0], w_value[0], w_out[0], w_up[0], w_down[0],
        final_gain[None, :],
    )
    weight = conv_weight.reshape(-1, conv_weight.shape[3])
    return conv_image(final, row, col, corner, weight)


def solution(mesh):
    sizes = (mesh.shape["row"], mesh.shape["col"])
    return jax.shard_map(
        functools.partial(local, sizes),
        mesh=mesh,
        in_specs=(P("row", "col", None), P(), P(), P(), P(), P(), P(), P(), P(), P()),
        out_specs=P(None, "row", "col"),
        check_vma=False,
    )
```

profile of v0, /device:TPU:11, one launch (start us, length us, event | category | flops | bytes accessed | tf_op | source)
XLA Modules:
  0.0 40.5 jit_solution(11866528791742913132)
XLA Ops:
  0.0 36.3 %layer.1 = (bf16[24,32,256]{2,1,0:T(8,128)(2,1)}, bf16[2,32,256]{2,1,0:T(8,128)(2,1)}, bf16[2,24,256]{2,1,0:T(8,128)(2,1)}, bf16[4,8,256]{2,1,0:T(8,128)(2,1)}) custom-call(bf16[24,4,8,256]{3,2,1,0:T(8,128)(2,1)} %bitcast.13, f32[2,256]{1,0:T(2,128)} %bitcast.18, bf16[256,256]{1,0:T(8,128)(2,1)} %bitcast.14, bf16[256,256]{1,0:T(8,128)(2,1)} %bitcast.15, ...), custom_call_target="tpu_custom_call" | custom-call | tf_op jit(solution)/shard_map/layer/pallas_call | solution.py:249
  36.3 4.1 %conv_image.1 = f32[16,96,128]{2,1,0:T(8,128)} custom-call(bf16[24,32,256]{2,1,0:T(8,128)(2,1)} %get-tuple-element.9.final_ref, bf16[2,32,256]{2,1,0:T(8,128)(2,1)} %get-tuple-element.10.row_h, bf16[2,24,256]{2,1,0:T(8,128)(2,1)} %get-tuple-element.11.col_h, bf16[4,8,256]{2,1,0:T(8,128)(2,1)} %get-tuple-element.12.cor_h, bf16[2304,256]{1,0:T(8,128)(2,1)} %bitcast.10), custom_call_target="tpu_custom_call" | custom-call | tf_op jit(solution)/shard_map/conv_image/pallas_call | solution.py:341
where the time goes:
time: 41.2 us; the launch traced here: 40.5 us
  Pallas kernels  40.5 us (98%)
    pallas_call x1, Pallas kernels, layer(): pl.pallas_call(functools.partial(layer_kernel, sizes), out_shape=(jax.Sha...  36.3 us
    pallas_call x1, Pallas kernels, conv_image(): pl.pallas_call(conv_kernel, out_shape=jax.ShapeDtypeStruct((outs // SHUF...  4.14 us

commit v1 on v0

--- a/solution.py
+++ b/solution.py
@@ -11,6 +11,8 @@
 HALO = 8
 SHUF = 4
 CHUNK = 256
+STEP = 128
+TAIL = 16
 VMEM_LIMIT = 56 * 1024 * 1024
 BF = jnp.bfloat16
 F32 = jnp.float32
@@ -107,16 +109,20 @@
     return swap(sizes, sources, slots, send, recv, fills)
 
 
+def nt_dot(left, right):
+    return lax.dot_general(left, right, (((1,), (1,)), ((), ())), preferred_element_type=F32)
+
+
 def layer_kernel(
     sizes,
     field_ref, gains_ref, wq_ref, wk_ref, wv_ref, wo_hbm, wu_hbm, wd_hbm, fg_ref,
     out_ref, row_h, col_h, cor_h,
-    halo_ref, q_s, kt_s, va_s, f_s, o_s, m_s, left_s, right_s, wo_ref, wu_ref, wd_ref,
+    halo_ref, qt_s, k_s, va_s, s_s, o_s, m_s, f_s, left_s, right_s, wo_ref, wu_ref, wd_ref,
     send, recv, send2, recv2, wsem,
 ):
     rows, groups = field_ref.shape[:2]
     cols = groups * 8
-    tokens, width = q_s.shape
+    width, tokens = qt_s.shape
     head = width // HEADS
     per = 128 // head
     loads = [
@@ -131,47 +137,85 @@
     g0 = gains_ref[0:1, :]
     g1 = gains_ref[1:2, :]
     fg = fg_ref[...]
-    lane = lax.broadcasted_iota(jnp.int32, (1, 128), 1) // head
+    wqt = wq_ref[...].T
+    wvt = wv_ref[...].T
 
     def keep(h, start, ok):
-        k = jnp.dot(h, wk_ref[...], preferred_element_type=F32)
-        kt_s[:, start : start + h.shape[0]] = k.T.astype(BF)
-        v = jnp.dot(h, wv_ref[...], preferred_element_type=F32)
+        count = h.shape[0]
+        keys = slice(start, start + count)
+        k_s[keys, :] = jnp.dot(h, wk_ref[...], preferred_element_type=F32).astype(BF)
+        v = nt_dot(wvt, h)
+        one = jnp.ones((TAIL, count), F32)
+        if ok is not None:
+            v = v * ok
+            one = one * ok
+        v = v.astype(BF)
+        one = one.astype(BF)
         for e in range(HEADS):
-            half = e // per
-            part = jnp.where(lane == e % per, v[:, half * 128 : half * 128 + 128], 1.0)
-            if ok is not None:
-                part = part * ok
-            va_s[e, start : start + h.shape[0], :] = part.astype(BF)
+            va_s[e, 0:head, keys] = v[e * head : (e + 1) * head]
+            va_s[e, head : head + TAIL, keys] = one
 
     scale = head**-0.5 * 1.4426950408889634
     span = CHUNK // cols
     for start in range(0, tokens, CHUNK):
         at = start // cols
         h = rms(field_ref[at : at + span].astype(F32).reshape(CHUNK, width), g0).astype(BF)
-        q = jnp.dot(h, wq_ref[...], preferred_element_type=F32) * scale
-        q_s[start : start + CHUNK, :] = q.astype(BF)
+        qt_s[:, start : start + CHUNK] = (nt_dot(wqt, h) * scale).astype(BF)
         keep(h, start, None)
 
-    def head_part(at, half, e, first, count):
-        qh = q_s[at, half * 128 : half * 128 + 128]
-        qm = jnp.where(lane == e, qh, jnp.zeros_like(qh))
-        keys = slice(first, first + count)
-        s = jnp.dot(qm, kt_s[half * 128 : half * 128 + 128, keys], preferred_element_type=F32)
-        m = jnp.max(s, axis=-1, keepdims=True)
-        p = jnp.exp2((s - m).astype(BF))
-        return m, jnp.dot(p, va_s[half * per + e, keys, :], preferred_element_type=F32)
-
-    def own(index, carry):
-        at = pl.ds(pl.multiple_of(index * CHUNK, CHUNK), CHUNK)
-        for half in range(width // 128):
-            for e in range(per):
-                m, o = head_part(at, half, e, 0, tokens)
-                o_s[half * per + e, at, :] = o
-                m_s[half * per + e, at, :] = jnp.broadcast_to(m, o.shape)
-        return carry
-
-    lax.fori_loop(0, tokens // CHUNK, own, 0)
+    def scores(item, slot, first, count, base):
+        start, e = item
+        half, sub = e // per, e % per
+        zero = jnp.zeros((head, CHUNK), BF)
+        q = qt_s[e * head : (e + 1) * head, start : start + CHUNK]
+        q = jnp.concatenate([q if n == sub else zero for n in range(per)], axis=0)
+        top = base
+        for kc in range(0, count, STEP):
+            s = jnp.dot(
+                k_s[first + kc : first + kc + STEP, half * 128 : half * 128 + 128], q,
+                preferred_element_type=F32,
+            )
+            s_s[slot, kc : kc + STEP, :] = s
+            part = jnp.max(s.reshape(STEP // 8, 8, CHUNK), axis=0)
+            top = part if top is None else jnp.maximum(top, part)
+            yield None
+        top = jnp.max(top, axis=0, keepdims=True)
+        yield top
+
+    def values(item, slot, first, count, top):
+        start, e = item
+        acc = None
+        for kc in range(0, count, STEP):
+            p = jnp.exp2((s_s[slot, kc : kc + STEP, :] - top).astype(BF))
+            o = jnp.dot(
+                va_s[e, :, first + kc : first + kc + STEP], p, preferred_element_type=F32
+            )
+            acc = o if acc is None else acc + o
+            yield None
+        yield acc
+
+    def attend(items, first, count, base, done):
+        before = None
+        for n, item in enumerate(items + [None]):
+            slot = n % 2
+            now = None if item is None else scores(item, slot, first, count, base(item))
+            then = None if before is None else values(before[0], 1 - slot, first, count, before[1])
+            top = acc = None
+            for _ in range(count // STEP + 1):
+                top = top if now is None else next(now)
+                acc = acc if then is None else next(then)
+            if before is not None:
+                done(before[0], before[1], acc)
+            before = (item, top)
+
+    items = [(start, e) for start in range(0, tokens, CHUNK) for e in range(HEADS)]
+
+    def own_done(item, top, acc):
+        start, e = item
+        o_s[e, :, start : start + CHUNK] = acc
+        m_s[e, :, start : start + CHUNK] = jnp.broadcast_to(top, (8, CHUNK))
+
+    attend(items, 0, tokens, lambda item: None, own_done)
     finish(copies)
 
     first = 0
@@ -184,40 +228,42 @@
     for start in range(0, total, 128):
         raw = halo_ref[start // 8 : start // 8 + 16].astype(F32).reshape(128, width)
         h = rms(raw, g0).astype(BF)
-        row = lax.broadcasted_iota(jnp.int32, (128, 1), 0) + start
-        ok = jnp.zeros((128, 1), F32)
+        spot = lax.broadcasted_iota(jnp.int32, (1, 128), 1) + start
+        ok = jnp.zeros((1, 128), F32)
         for at, count, flag in marks:
             if at < start + 128 and at + count > start:
-                ok = jnp.where((row >= at) & (row < at + count), flag, ok)
+                ok = jnp.where((spot >= at) & (spot < at + count), flag, ok)
         keep(h, tokens + start, ok)
     for load in loads:
         load.wait()
 
-    def body(index, carry):
-        at = pl.ds(pl.multiple_of(index * CHUNK, CHUNK), CHUNK)
-        halves = []
-        for half in range(width // 128):
-            ctx = jnp.zeros((CHUNK, 128), F32)
-            for e in range(per):
-                m, o = head_part(at, half, e, tokens, total)
-                old = m_s[half * per + e, at, :]
-                top = jnp.maximum(old, m)
-                o = o * jnp.exp2(m - top) + o_s[half * per + e, at, :] * jnp.exp2(old - top)
-                ctx = jnp.where(lane == e, o / pltpu.roll(o, head, 1), ctx)
-            halves.append(ctx.astype(BF))
-        ctx = jnp.concatenate(halves, axis=1)
-        x = field_ref[pl.ds(index * span, span)].astype(F32).reshape(CHUNK, width)
+    context = {}
+
+    def tail(start, ctx):
+        at = start // cols
+        x = field_ref[at : at + span].astype(F32).reshape(CHUNK, width)
         x = x + jnp.dot(ctx, wo_ref[...], preferred_element_type=F32)
         h = rms(x, g1).astype(BF)
         u = jax.nn.gelu(jnp.dot(h, wu_ref[...], preferred_element_type=F32)).astype(BF)
         x = x + jnp.dot(u, wd_ref[...], preferred_element_type=F32)
         f = rms(x, fg)
-        out_ref[pl.ds(index * span, span)] = f.reshape(span, cols, width).astype(BF)
+        out_ref[at : at + span] = f.reshape(span, cols, width).astype(BF)
         for half in range(width // 128):
-            f_s[half, at, :] = f[:, half * 128 : half * 128 + 128]
-        return carry
-
-    lax.fori_loop(0, tokens // CHUNK, body, 0)
+            f_s[half, start : start + CHUNK, :] = f[:, half * 128 : half * 128 + 128]
+
+    def all_done(item, top, acc):
+        start, e = item
+        old = m_s[e, 0:1, start : start + CHUNK]
+        acc = acc + o_s[e, :, start : start + CHUNK] * jnp.exp2(old - top)
+        context[e] = acc[0:head] / acc[head : head + 1]
+        if e == HEADS - 1:
+            ctx = jnp.concatenate([context[n] for n in range(HEADS)], axis=0)
+            tail(start, ctx.T.astype(BF))
+
+    attend(
+        items, tokens, total,
+        lambda item: m_s[item[1], :, item[0] : item[0] + CHUNK], all_done,
+    )
     for half in range(width // 128):
         sl = slice(half * 128, half * 128 + 128)
         left_s[:, sl] = f_s[half, pl.ds(0, rows, stride=cols), :].astype(BF)
@@ -258,12 +304,13 @@
         out_specs=(vm,) * 4,
         scratch_shapes=[
             pltpu.VMEM((blocks, 8, width), BF),
-            pltpu.VMEM((tokens, width), BF),
-            pltpu.VMEM((width, keys), BF),
-            pltpu.VMEM((HEADS, keys, 128), BF),
+            pltpu.VMEM((width, tokens), BF),
+            pltpu.VMEM((keys, width), BF),
+            pltpu.VMEM((HEADS, width // HEADS + TAIL, keys), BF),
+            pltpu.VMEM((2, max(tokens, keys - tokens), CHUNK), F32),
+            pltpu.VMEM((HEADS, width // HEADS + TAIL, tokens), F32),
+            pltpu.VMEM((HEADS, 8, tokens), F32),
             pltpu.VMEM((width // 128, tokens, 128), F32),
-            pltpu.VMEM((HEADS, tokens, 128), F32),
-            pltpu.VMEM((HEADS, tokens, 128), F32),
             pltpu.VMEM((rows, width), BF),
             pltpu.VMEM((rows, width), BF),
             pltpu.VMEM(wo.shape, BF),

time: 41.2 us -> 36.5 us (0.89); the launches traced: 40.5 us -> 36.4 us
  Pallas kernels: 40.5 us -> 36.4 us
    pallas_call x1, Pallas kernels: 36.3 us -> 32.2 us  [layer(): pl.pallas_call(functools.partial(layer_kernel, sizes), out_shape=(jax.Sha...]
where the time goes in v1:
time: 36.5 us; the launch traced here: 36.4 us
  Pallas kernels  36.4 us (100%)
    pallas_call x1, Pallas kernels, layer(): pl.pallas_call(functools.partial(layer_kernel, sizes), out_shape=(jax.Sha...  32.2 us
    pallas_call x1, Pallas kernels, conv_image(): pl.pallas_call(conv_kernel, out_shape=jax.ShapeDtypeStruct((outs // SHUF...  4.14 us

profile of v1, /device:TPU:11, one launch (start us, length us, event | category | flops | bytes accessed | tf_op | source)
XLA Modules:
  0.0 36.4 jit_solution(11782370320258075111)
XLA Ops:
  0.0 32.2 %layer.1 = (bf16[24,32,256]{2,1,0:T(8,128)(2,1)}, bf16[2,32,256]{2,1,0:T(8,128)(2,1)}, bf16[2,24,256]{2,1,0:T(8,128)(2,1)}, bf16[4,8,256]{2,1,0:T(8,128)(2,1)}) custom-call(bf16[24,4,8,256]{3,2,1,0:T(8,128)(2,1)} %bitcast.13, f32[2,256]{1,0:T(2,128)} %bitcast.18, bf16[256,256]{1,0:T(8,128)(2,1)} %bitcast.14, bf16[256,256]{1,0:T(8,128)(2,1)} %bitcast.15, ...), custom_call_target="tpu_custom_call" | custom-call | tf_op jit(solution)/shard_map/layer/pallas_call | solution.py:295
  32.2 4.1 %conv_image.1 = f32[16,96,128]{2,1,0:T(8,128)} custom-call(bf16[24,32,256]{2,1,0:T(8,128)(2,1)} %get-tuple-element.9.final_ref, bf16[2,32,256]{2,1,0:T(8,128)(2,1)} %get-tuple-element.10.row_h, bf16[2,24,256]{2,1,0:T(8,128)(2,1)} %get-tuple-element.11.col_h, bf16[4,8,256]{2,1,0:T(8,128)(2,1)} %get-tuple-element.12.cor_h, bf16[2304,256]{1,0:T(8,128)(2,1)} %bitcast.10), custom_call_target="tpu_custom_call" | custom-call | tf_op jit(solution)/shard_map/conv_image/pallas_call | solution.py:388
